TPU v7x, 512 devices: a whole 4x8x8 slice. The times are simulated.
512 devices in a mesh: cols: 64 (over z, x, y_hi), rows: 8 (over y_lo, core).
Axes of the slice: x: 4, y: 8 (y_hi: 2, y_lo: 4; y = y_hi * 4 + y_lo), z: 8, core: 2. Of those that a mesh axis runs over, the one named last changes fastest.
Arguments:
- vectors: float32 [8192, 16384], P('rows', 'cols'), may hold values from -6 to 6
- reflectors: float32 [15, 1024, 512], P(None, None, 'cols'), may hold values from -40 to 40, as said below
- factors: float32 [15, 512, 512], P(None, None, 'cols'), may hold values from -1 to 1
Outputs:
- result: float32 [8192, 16384], P('rows', 'cols')
Inputs may be any that keep to these rules, and one draw needn't show every extreme that they name: `reflectors`: column j of each block is zero outside its rows j to j + 511, and its entry in row j is 1.
All inputs are finite; a program needn't handle non-finite values.
Results may differ from a plain program's by a relative error of at most 0.00028.
Values sent between devices are 32-bit elements; how exact they have to be, the bound alone decides.
A program may use at most 64 MiB of HBM per device.

v0:
```python
import jax
import jax.numpy as jnp
from jax import lax
from jax.sharding import PartitionSpec as P


def rows_first(arrays, axis, dims):
    turned = [jnp.moveaxis(a, dim, 0) for a, dim in zip(arrays, dims)]
    both = jnp.concatenate([t.reshape(len(t), -1) for t in turned], axis=1)
    filled, at, outs = (lax.all_gather(both, axis, axis=0, tiled=True), 0, [])
    for t, dim in zip(turned, dims):
        slab = filled[:, at : at + t[0].size].reshape(-1, *t.shape[1:])
        outs.append(jnp.moveaxis(slab, 0, dim))
        at += t[0].size
    return tuple(outs)


def shifted(value, axis, by):
    length = lax.axis_size(axis)
    pairs = [(i, i + by) for i in range(length) if 0 <= i + by < length]
    return lax.ppermute(value, axis, pairs)


def reflect(window, basis_cols, factor):
    highest = lax.Precision.HIGHEST
    weights = lax.dot_general(
        basis_cols,
        window,
        (((0,), (0,)), ((), ())),
        precision=highest,
        preferred_element_type=jnp.float32,
    )
    coeffs = jnp.dot(factor, weights, precision=highest, preferred_element_type=jnp.float32)
    return window - jnp.dot(
        basis_cols, coeffs, precision=highest, preferred_element_type=jnp.float32
    )


def body(vectors, reflectors, factors):
    row_count = lax.axis_size("rows")
    row_index = lax.axis_index("rows")
    rows_dev, cols_dev = vectors.shape
    half_rows = rows_dev // 2
    first_index = jnp.maximum(2 * row_index - 1, 0)
    own_index = 2 * row_index
    upper_basis = lax.dynamic_index_in_dim(reflectors, first_index, 0, keepdims=False)
    upper_factor = lax.dynamic_index_in_dim(factors, first_index, 0, keepdims=False)
    own_basis = lax.dynamic_index_in_dim(reflectors, own_index, 0, keepdims=False)
    own_factor = lax.dynamic_index_in_dim(factors, own_index, 0, keepdims=False)
    pair_basis = jnp.stack([upper_basis, own_basis])
    pair_factor = jnp.stack([upper_factor, own_factor])
    full_basis, full_factor = rows_first((pair_basis, pair_factor), "cols", (2, 2))
    upper_basis, own_basis = (full_basis[0], full_basis[1])
    upper_factor, own_factor = (full_factor[0], full_factor[1])
    stripe_count = 2
    stripe_cols = cols_dev // stripe_count
    has_upper = row_index > 0
    has_lower = row_index < row_count - 1

    def process(state_now, incoming, stripe_index):
        matrix, outgoing, returning = state_now
        start = stripe_index * stripe_cols
        stripe = lax.dynamic_slice_in_dim(matrix, start, stripe_cols, 1)
        window = reflect(
            jnp.concatenate([incoming, stripe[:half_rows]], 0), upper_basis, upper_factor
        )
        upper_rows = jnp.where(has_upper, window[half_rows:], stripe[:half_rows])
        stripe = reflect(
            jnp.concatenate([upper_rows, stripe[half_rows:]], 0), own_basis, own_factor
        )
        matrix = lax.dynamic_update_slice_in_dim(matrix, stripe, start, 1)
        return (matrix, stripe[half_rows:], window[:half_rows])

    def advance(turn_index, state_now):
        matrix, outgoing, returning = state_now
        incoming = shifted(outgoing, "rows", 1)
        arrived = shifted(returning, "rows", -1)
        late_stripe = turn_index - row_index - 2
        landing = (late_stripe >= 0) & (late_stripe < stripe_count) & has_lower
        late_start = jnp.clip(late_stripe, 0, stripe_count - 1) * stripe_cols
        current = lax.dynamic_slice(matrix, (half_rows, late_start), (half_rows, stripe_cols))
        matrix = lax.dynamic_update_slice(
            matrix, jnp.where(landing, arrived, current), (half_rows, late_start)
        )
        stripe_index = turn_index - row_index
        is_active = (stripe_index >= 0) & (stripe_index < stripe_count)
        safe_index = jnp.clip(stripe_index, 0, stripe_count - 1)

        def busy(state_in):
            return process(state_in, incoming, safe_index)

        def resting(state_in):
            return state_in

        return lax.cond(is_active, busy, resting, (matrix, outgoing, returning))

    blank = jnp.zeros((half_rows, stripe_cols), jnp.float32)
    matrix, outgoing, returning = lax.fori_loop(
        0, row_count + stripe_count, advance, (vectors, blank, blank)
    )
    return matrix


def solution(mesh):
    placed = (P("rows", "cols"), P(None, None, "cols"), P(None, None, "cols"))
    return jax.shard_map(
        body, mesh=mesh, in_specs=placed, out_specs=P("rows", "cols"), check_vma=False
    )
```

profile of v0, /device:TPU:25, one launch (start us, length us, event | category | flops | bytes accessed | tf_op | source)
XLA Modules:
  0.0 437.3 jit_solution(806147630762032506)
XLA Ops:
  8.8 2.6 copy.8
  11.3 166.3 %all-gather.2.cloned.1.call-done = f32[512,3072]{1,0:T(8,128)} async-done(((f32[8,3072]{1,0:T(8,128)}), f32[512,3072]{1,0:T(8,128)}) %all-gather.2.cloned.1.call-update) | async-done | bytes 6291472 | tf_op jit(solution)/shard_map/all_gather | solution.py:10
  177.6 4.8 %slice.43 = f32[512,2048]{1,0:T(8,128)} slice(f32[512,3072]{1,0:T(8,128)} %all-gather.2.cloned.1.call-done), slice={[0:512], [0:2048]} | slice | bytes 8388608 | tf_op jit(solution)/shard_map/slice | solution.py:12
  182.4 5.4 %copy.10 = f32[512,2048]{0,1:T(8,128)} copy(f32[512,2048]{1,0:T(8,128)} %slice.43) | data formatting | bytes 8388608 | tf_op jit(solution)/shard_map/reshape | solution.py:12
  187.8 3.2 slice.45
  190.9 1.9 copy.11
  194.0 1.4 copy-done.4
  195.4 1.8 slice_bitcast_fusion
  198.6 229.3 %while.19 = (s32[]{:T(128)}, f32[1024,256]{0,1:T(8,128)}, f32[512,128]{0,1:T(8,128)}, f32[512,128]{0,1:T(8,128)}, s32[]{:T(128)}, /*index=5*/pred[]{:T(512)}, pr...) while((s32[]{:T(128)}, f32[1024,256]{0,1:T(8,128)}, ...), condition=%wide.region_3.4_spmd, body=%wide.region_0.3_spmd.sunk | while | flops 4027449344 | bytes 42992328 | solution.py:98
  198.6 6.5 %collective-permute-start = (f32[512,128]{0,1:T(8,128)}, f32[512,128]{0,1:T(8,128)}, u32[]{:S(2)}, u32[]{:S(2)}) collective-permute-start(f32[512,128]{0,1:T(8,128)} %get-tuple-element.479), channel_id=1, source_target_pairs={{1,0},{2,1},{3,2},{4,3},{5,4},{6,5},{7,6},{9,8},{10,9},{11,10},{12... | collective-permute-start | bytes 786440 | tf_op jit(solution)/shard_map/while/body/eval_jaxpr/ppermute | solution.py:21
  205.1 1.3 collective-permute-start.1
  206.4 1.7 select_dynamic-update-slice_fusion.2
  208.2 2.4 collective-permute-done.1
  210.5 9.5 %collective-permute-start = (f32[512,128]{0,1:T(8,128)}, f32[512,128]{0,1:T(8,128)}, u32[]{:S(2)}, u32[]{:S(2)}) collective-permute-start(f32[512,128]{0,1:T(8,128)} %get-tuple-element.479), channel_id=1, source_target_pairs={{1,0},{2,1},{3,2},{4,3},{5,4},{6,5},{7,6},{9,8},{10,9},{11,10},{12... | collective-permute-start | bytes 786440 | tf_op jit(solution)/shard_map/while/body/eval_jaxpr/ppermute | solution.py:21
  220.0 1.3 collective-permute-start.1
  221.4 1.7 select_dynamic-update-slice_fusion.2
  223.7 6.3 %collective-permute-start = (f32[512,128]{0,1:T(8,128)}, f32[512,128]{0,1:T(8,128)}, u32[]{:S(2)}, u32[]{:S(2)}) collective-permute-start(f32[512,128]{0,1:T(8,128)} %get-tuple-element.479), channel_id=1, source_target_pairs={{1,0},{2,1},{3,2},{4,3},{5,4},{6,5},{7,6},{9,8},{10,9},{11,10},{12... | collective-permute-start | bytes 786440 | tf_op jit(solution)/shard_map/while/body/eval_jaxpr/ppermute | solution.py:21
  230.0 1.3 collective-permute-start.1
  231.3 1.7 select_dynamic-update-slice_fusion.2
  233.6 6.2 %collective-permute-start = (f32[512,128]{0,1:T(8,128)}, f32[512,128]{0,1:T(8,128)}, u32[]{:S(2)}, u32[]{:S(2)}) collective-permute-start(f32[512,128]{0,1:T(8,128)} %get-tuple-element.479), channel_id=1, source_target_pairs={{1,0},{2,1},{3,2},{4,3},{5,4},{6,5},{7,6},{9,8},{10,9},{11,10},{12... | collective-permute-start | bytes 786440 | tf_op jit(solution)/shard_map/while/body/eval_jaxpr/ppermute | solution.py:21
  239.8 1.3 collective-permute-start.1
  241.1 1.7 select_dynamic-update-slice_fusion.2
  243.4 16.8 %collective-permute-start = (f32[512,128]{0,1:T(8,128)}, f32[512,128]{0,1:T(8,128)}, u32[]{:S(2)}, u32[]{:S(2)}) collective-permute-start(f32[512,128]{0,1:T(8,128)} %get-tuple-element.479), channel_id=1, source_target_pairs={{1,0},{2,1},{3,2},{4,3},{5,4},{6,5},{7,6},{9,8},{10,9},{11,10},{12... | collective-permute-start | bytes 786440 | tf_op jit(solution)/shard_map/while/body/eval_jaxpr/ppermute | solution.py:21
  261.5 1.7 select_dynamic-update-slice_fusion.2
  263.2 7.7 %collective-permute-done.1 = f32[512,128]{0,1:T(8,128)S(1)} collective-permute-done((f32[512,128]{0,1:T(8,128)}, f32[512,128]{0,1:T(8,128)S(1)}, u32[]{:S(2)}, u32[]{:S(2)}) %collective-permute-start.1) | collective-permute-done | bytes 262176 | tf_op jit(solution)/shard_map/while/body/eval_jaxpr/ppermute | solution.py:21
  270.9 28.4 %collective-permute-start = (f32[512,128]{0,1:T(8,128)}, f32[512,128]{0,1:T(8,128)}, u32[]{:S(2)}, u32[]{:S(2)}) collective-permute-start(f32[512,128]{0,1:T(8,128)} %get-tuple-element.479), channel_id=1, source_target_pairs={{1,0},{2,1},{3,2},{4,3},{5,4},{6,5},{7,6},{9,8},{10,9},{11,10},{12... | collective-permute-start | bytes 786440 | tf_op jit(solution)/shard_map/while/body/eval_jaxpr/ppermute | solution.py:21
  300.6 1.7 select_dynamic-update-slice_fusion.2
  302.4 10.7 %collective-permute-done.1 = f32[512,128]{0,1:T(8,128)S(1)} collective-permute-done((f32[512,128]{0,1:T(8,128)}, f32[512,128]{0,1:T(8,128)S(1)}, u32[]{:S(2)}, u32[]{:S(2)}) %collective-permute-start.1) | collective-permute-done | bytes 262176 | tf_op jit(solution)/shard_map/while/body/eval_jaxpr/ppermute | solution.py:21
  313.1 26.0 %collective-permute-start = (f32[512,128]{0,1:T(8,128)}, f32[512,128]{0,1:T(8,128)}, u32[]{:S(2)}, u32[]{:S(2)}) collective-permute-start(f32[512,128]{0,1:T(8,128)} %get-tuple-element.479), channel_id=1, source_target_pairs={{1,0},{2,1},{3,2},{4,3},{5,4},{6,5},{7,6},{9,8},{10,9},{11,10},{12... | collective-permute-start | bytes 786440 | tf_op jit(solution)/shard_map/while/body/eval_jaxpr/ppermute | solution.py:21
  340.4 1.7 select_dynamic-update-slice_fusion.2
  342.1 13.7 %collective-permute-done.1 = f32[512,128]{0,1:T(8,128)S(1)} collective-permute-done((f32[512,128]{0,1:T(8,128)}, f32[512,128]{0,1:T(8,128)S(1)}, u32[]{:S(2)}, u32[]{:S(2)}) %collective-permute-start.1) | collective-permute-done | bytes 262176 | tf_op jit(solution)/shard_map/while/body/eval_jaxpr/ppermute | solution.py:21
  355.9 23.0 %collective-permute-start = (f32[512,128]{0,1:T(8,128)}, f32[512,128]{0,1:T(8,128)}, u32[]{:S(2)}, u32[]{:S(2)}) collective-permute-start(f32[512,128]{0,1:T(8,128)} %get-tuple-element.479), channel_id=1, source_target_pairs={{1,0},{2,1},{3,2},{4,3},{5,4},{6,5},{7,6},{9,8},{10,9},{11,10},{12... | collective-permute-start | bytes 786440 | tf_op jit(solution)/shard_map/while/body/eval_jaxpr/ppermute | solution.py:21
  380.2 1.7 select_dynamic-update-slice_fusion.2
  382.5 15.0 %conditional.2 = ((f32[1024,256]{0,1:T(8,128)}, f32[512,128]{0,1:T(8,128)}, f32[512,128]{0,1:T(8,128)})) conditional(s32[]{:T(128)} %convert_element_type.11, (f32[1024,256]{0,1:T(8,128)}, f32[512,128]{0,1:T(8,128)}, f32[512,128]{0,1:T(8,128)}) %tuple.54, (pred[]{:T(512)}, s32[]{:T(128)}, f32[1024,256]{0,1:T(8,128)}, f32[512,128]{0,1:T(8,128)S(1)}, ...), branch_computations={%region_1.1_spmd, %region_2.2_spmd} | conditional | flops 4027383808 | bytes 40108272 | solution.py:95
  383.7 3.0 fusion.3
  387.9 2.3 fusion
  391.0 1.3 fusion.2
  393.5 2.3 constant_dynamic-update-slice_fusion
  397.5 6.2 %collective-permute-start = (f32[512,128]{0,1:T(8,128)}, f32[512,128]{0,1:T(8,128)}, u32[]{:S(2)}, u32[]{:S(2)}) collective-permute-start(f32[512,128]{0,1:T(8,128)} %get-tuple-element.479), channel_id=1, source_target_pairs={{1,0},{2,1},{3,2},{4,3},{5,4},{6,5},{7,6},{9,8},{10,9},{11,10},{12... | collective-permute-start | bytes 786440 | tf_op jit(solution)/shard_map/while/body/eval_jaxpr/ppermute | solution.py:21
  405.0 1.7 select_dynamic-update-slice_fusion.2
  407.3 15.0 %conditional.2 = ((f32[1024,256]{0,1:T(8,128)}, f32[512,128]{0,1:T(8,128)}, f32[512,128]{0,1:T(8,128)})) conditional(s32[]{:T(128)} %convert_element_type.11, (f32[1024,256]{0,1:T(8,128)}, f32[512,128]{0,1:T(8,128)}, f32[512,128]{0,1:T(8,128)}) %tuple.54, (pred[]{:T(512)}, s32[]{:T(128)}, f32[1024,256]{0,1:T(8,128)}, f32[512,128]{0,1:T(8,128)S(1)}, ...), branch_computations={%region_1.1_spmd, %region_2.2_spmd} | conditional | flops 4027383808 | bytes 40108272 | solution.py:95
  408.5 3.0 fusion.3
  412.7 2.3 fusion
  415.8 1.3 fusion.2
  418.3 2.3 constant_dynamic-update-slice_fusion
  422.3 2.0 collective-permute-start
  425.7 1.7 select_dynamic-update-slice_fusion.2
  428.0 2.5 copy.9
  (67 shorter events, 28.0 us)
Async XLA Ops:
  6.5 171.1 %all-gather.2.cloned.1.call-start = ((), (), s32[]{:S(2)}) async-start(), calls=%async_computation | async-start | bytes 6389760 | tf_op jit(solution)/shard_map/all_gather | solution.py:10
  192.9 2.6 copy-start.4
  198.6 7.8 %collective-permute-start = (f32[512,128]{0,1:T(8,128)}, f32[512,128]{0,1:T(8,128)}, u32[]{:S(2)}, u32[]{:S(2)}) collective-permute-start(f32[512,128]{0,1:T(8,128)} %get-tuple-element.479), channel_id=1, source_target_pairs={{1,0},{2,1},{3,2},{4,3},{5,4},{6,5},{7,6},{9,8},{10,9},{11,10},{12... | collective-permute-start | bytes 786440 | tf_op jit(solution)/shard_map/while/body/eval_jaxpr/ppermute | solution.py:21
  205.1 5.4 %collective-permute-start.1 = (f32[512,128]{0,1:T(8,128)}, f32[512,128]{0,1:T(8,128)S(1)}, u32[]{:S(2)}, u32[]{:S(2)}) collective-permute-start(f32[512,128]{0,1:T(8,128)} %get-tuple-element.478), channel_id=1, source_target_pairs={{0,1},{1,2},{2,3},{3,4},{4,5},{5,6},{6,7},{8,9},{9,10},{10,11},{11... | collective-permute-start | bytes 786440 | tf_op jit(solution)/shard_map/while/body/eval_jaxpr/ppermute | solution.py:21
  210.5 10.8 %collective-permute-start = (f32[512,128]{0,1:T(8,128)}, f32[512,128]{0,1:T(8,128)}, u32[]{:S(2)}, u32[]{:S(2)}) collective-permute-start(f32[512,128]{0,1:T(8,128)} %get-tuple-element.479), channel_id=1, source_target_pairs={{1,0},{2,1},{3,2},{4,3},{5,4},{6,5},{7,6},{9,8},{10,9},{11,10},{12... | collective-permute-start | bytes 786440 | tf_op jit(solution)/shard_map/while/body/eval_jaxpr/ppermute | solution.py:21
  220.0 3.6 collective-permute-start.1
  223.7 7.6 %collective-permute-start = (f32[512,128]{0,1:T(8,128)}, f32[512,128]{0,1:T(8,128)}, u32[]{:S(2)}, u32[]{:S(2)}) collective-permute-start(f32[512,128]{0,1:T(8,128)} %get-tuple-element.479), channel_id=1, source_target_pairs={{1,0},{2,1},{3,2},{4,3},{5,4},{6,5},{7,6},{9,8},{10,9},{11,10},{12... | collective-permute-start | bytes 786440 | tf_op jit(solution)/shard_map/while/body/eval_jaxpr/ppermute | solution.py:21
  230.0 3.6 collective-permute-start.1
  233.6 7.5 %collective-permute-start = (f32[512,128]{0,1:T(8,128)}, f32[512,128]{0,1:T(8,128)}, u32[]{:S(2)}, u32[]{:S(2)}) collective-permute-start(f32[512,128]{0,1:T(8,128)} %get-tuple-element.479), channel_id=1, source_target_pairs={{1,0},{2,1},{3,2},{4,3},{5,4},{6,5},{7,6},{9,8},{10,9},{11,10},{12... | collective-permute-start | bytes 786440 | tf_op jit(solution)/shard_map/while/body/eval_jaxpr/ppermute | solution.py:21
  239.8 3.6 collective-permute-start.1
  243.4 18.1 %collective-permute-start = (f32[512,128]{0,1:T(8,128)}, f32[512,128]{0,1:T(8,128)}, u32[]{:S(2)}, u32[]{:S(2)}) collective-permute-start(f32[512,128]{0,1:T(8,128)} %get-tuple-element.479), channel_id=1, source_target_pairs={{1,0},{2,1},{3,2},{4,3},{5,4},{6,5},{7,6},{9,8},{10,9},{11,10},{12... | collective-permute-start | bytes 786440 | tf_op jit(solution)/shard_map/while/body/eval_jaxpr/ppermute | solution.py:21
  260.2 10.7 %collective-permute-start.1 = (f32[512,128]{0,1:T(8,128)}, f32[512,128]{0,1:T(8,128)S(1)}, u32[]{:S(2)}, u32[]{:S(2)}) collective-permute-start(f32[512,128]{0,1:T(8,128)} %get-tuple-element.478), channel_id=1, source_target_pairs={{0,1},{1,2},{2,3},{3,4},{4,5},{5,6},{6,7},{8,9},{9,10},{10,11},{11... | collective-permute-start | bytes 786440 | tf_op jit(solution)/shard_map/while/body/eval_jaxpr/ppermute | solution.py:21
  270.9 29.7 %collective-permute-start = (f32[512,128]{0,1:T(8,128)}, f32[512,128]{0,1:T(8,128)}, u32[]{:S(2)}, u32[]{:S(2)}) collective-permute-start(f32[512,128]{0,1:T(8,128)} %get-tuple-element.479), channel_id=1, source_target_pairs={{1,0},{2,1},{3,2},{4,3},{5,4},{6,5},{7,6},{9,8},{10,9},{11,10},{12... | collective-permute-start | bytes 786440 | tf_op jit(solution)/shard_map/while/body/eval_jaxpr/ppermute | solution.py:21
  299.3 13.8 %collective-permute-start.1 = (f32[512,128]{0,1:T(8,128)}, f32[512,128]{0,1:T(8,128)S(1)}, u32[]{:S(2)}, u32[]{:S(2)}) collective-permute-start(f32[512,128]{0,1:T(8,128)} %get-tuple-element.478), channel_id=1, source_target_pairs={{0,1},{1,2},{2,3},{3,4},{4,5},{5,6},{6,7},{8,9},{9,10},{10,11},{11... | collective-permute-start | bytes 786440 | tf_op jit(solution)/shard_map/while/body/eval_jaxpr/ppermute | solution.py:21
  313.1 27.4 %collective-permute-start = (f32[512,128]{0,1:T(8,128)}, f32[512,128]{0,1:T(8,128)}, u32[]{:S(2)}, u32[]{:S(2)}) collective-permute-start(f32[512,128]{0,1:T(8,128)} %get-tuple-element.479), channel_id=1, source_target_pairs={{1,0},{2,1},{3,2},{4,3},{5,4},{6,5},{7,6},{9,8},{10,9},{11,10},{12... | collective-permute-start | bytes 786440 | tf_op jit(solution)/shard_map/while/body/eval_jaxpr/ppermute | solution.py:21
  339.1 16.8 %collective-permute-start.1 = (f32[512,128]{0,1:T(8,128)}, f32[512,128]{0,1:T(8,128)S(1)}, u32[]{:S(2)}, u32[]{:S(2)}) collective-permute-start(f32[512,128]{0,1:T(8,128)} %get-tuple-element.478), channel_id=1, source_target_pairs={{0,1},{1,2},{2,3},{3,4},{4,5},{5,6},{6,7},{8,9},{9,10},{10,11},{11... | collective-permute-start | bytes 786440 | tf_op jit(solution)/shard_map/while/body/eval_jaxpr/ppermute | solution.py:21
  355.9 24.3 %collective-permute-start = (f32[512,128]{0,1:T(8,128)}, f32[512,128]{0,1:T(8,128)}, u32[]{:S(2)}, u32[]{:S(2)}) collective-permute-start(f32[512,128]{0,1:T(8,128)} %get-tuple-element.479), channel_id=1, source_target_pairs={{1,0},{2,1},{3,2},{4,3},{5,4},{6,5},{7,6},{9,8},{10,9},{11,10},{12... | collective-permute-start | bytes 786440 | tf_op jit(solution)/shard_map/while/body/eval_jaxpr/ppermute | solution.py:21
  378.9 3.6 collective-permute-start.1
  382.5 4.2 copy-start.1
  383.7 4.2 copy-start
  391.0 2.5 copy-start.2
  395.8 1.0 copy-start.3
  397.5 7.5 %collective-permute-start = (f32[512,128]{0,1:T(8,128)}, f32[512,128]{0,1:T(8,128)}, u32[]{:S(2)}, u32[]{:S(2)}) collective-permute-start(f32[512,128]{0,1:T(8,128)} %get-tuple-element.479), channel_id=1, source_target_pairs={{1,0},{2,1},{3,2},{4,3},{5,4},{6,5},{7,6},{9,8},{10,9},{11,10},{12... | collective-permute-start | bytes 786440 | tf_op jit(solution)/shard_map/while/body/eval_jaxpr/ppermute | solution.py:21
  403.7 3.6 collective-permute-start.1
  407.3 4.2 copy-start.1
  408.5 4.2 copy-start
  415.8 2.5 copy-start.2
  420.6 1.0 copy-start.3
  422.3 3.3 collective-permute-start
  424.3 3.6 collective-permute-start.1
Sparse Core Ops, SparseCore 0:
  11.9 165.7 all-gather.1
where the time goes:
time: 439 us; the launch traced here: 437 us
  waiting for transfers between devices  204 us (46%)
  starting transfers between devices  144 us (33%)
  local copies, waits for them, and re-layouts  33.4 us (8%)
  matrix products  22.5 us (5%)
  other arithmetic  19.3 us (4%)
  between operations  13.4 us (3%)
    all_gather x1, waiting for transfers between devices, rows_first(): filled, at, outs = (lax.all_gather(both, axis, axis=0, tiled=True), 0, [])  166 us
    ppermute x20, starting transfers between devices, shifted(): return lax.ppermute(value, axis, pairs)  144 us
    ppermute x20, waiting for transfers between devices, shifted(): return lax.ppermute(value, axis, pairs)  38.1 us
    dynamic_update_slice x10, other arithmetic, advance(): lax.dynamic_update_slice(matrix, jnp.where(landing, arrived, current), (h...  17.1 us
    dot_general x4, matrix products, reflect(): jnp.dot(basis_cols, coeffs, precision=highest, preferred_element_type=jnp...  9.19 us
  transfers between devices with their start and end apart: 21, of which 11 were waited for; matrix products, arithmetic and copies ran while one was open for 5% of the time, Pallas kernels for 0%

commit v1 on v0

--- a/solution.py
+++ b/solution.py
@@ -7,7 +7,13 @@
 def rows_first(arrays, axis, dims):
     turned = [jnp.moveaxis(a, dim, 0) for a, dim in zip(arrays, dims)]
     both = jnp.concatenate([t.reshape(len(t), -1) for t in turned], axis=1)
-    filled, at, outs = (lax.all_gather(both, axis, axis=0, tiled=True), 0, [])
+    filled, at, outs = (
+        jnp.concatenate(
+            lax.all_to_all(jnp.stack([both] * lax.axis_size(axis)), axis, 0, 0), axis=0
+        ),
+        0,
+        [],
+    )
     for t, dim in zip(turned, dims):
         slab = filled[:, at : at + t[0].size].reshape(-1, *t.shape[1:])
         outs.append(jnp.moveaxis(slab, 0, dim))

time: 439 us -> 424 us (0.966)
  the two profiles are of different devices: /device:TPU:25 before, /device:TPU:121 now
where the time goes in v1:
time: 424 us; the launch traced here: 423 us
  waiting for transfers between devices  198 us (47%)
  starting transfers between devices  149 us (35%)
  local copies, waits for them, and re-layouts  34.4 us (8%)
  matrix products  22.6 us (5%)
  other arithmetic  18.8 us (4%)
    all_to_all x1, waiting for transfers between devices, rows_first(): lax.all_to_all(jnp.stack([both] * lax.axis_size(axis)), axis, 0, 0)  151 us
    ppermute x20, starting transfers between devices, shifted(): return lax.ppermute(value, axis, pairs)  131 us
    ppermute x20, waiting for transfers between devices, shifted(): return lax.ppermute(value, axis, pairs)  46.3 us
    all_to_all x1, starting transfers between devices, rows_first(): lax.all_to_all(jnp.stack([both] * lax.axis_size(axis)), axis, 0, 0)  17.5 us
    dynamic_update_slice x10, other arithmetic, advance(): lax.dynamic_update_slice(matrix, jnp.where(landing, arrived, current), (h...  17.3 us
    dot_general x4, matrix products, reflect(): jnp.dot(basis_cols, coeffs, precision=highest, preferred_element_type=jnp...  9.19 us
    dot_general x4, matrix products, reflect(): lax.dot_general(basis_cols, window, (((0,), (0,)), ((), ())), precision=h...  8.65 us
  transfers between devices with their start and end apart: 21, of which 11 were waited for; matrix products, arithmetic and copies ran while one was open for 4% of the time, Pallas kernels for 0%

profile of v1, /device:TPU:121, one launch (start us, length us, event | category | flops | bytes accessed | tf_op | source)
XLA Modules:
  0.0 423.0 jit_solution(5365069694602691470)
XLA Ops:
  1.6 3.4 stack.8
  4.9 17.5 %all-to-all-start = ((f32[64,8,3072]{2,1,0:T(8,128)}), f32[64,8,3072]{2,1,0:T(8,128)}, u32[]{:S(2)}, u32[]{:S(2)}) async-start(f32[64,8,3072]{2,1,0:T(8,128)} %stack.8), calls=%async_computation | async-start | bytes 12582912 | tf_op jit(solution)/shard_map/all_to_all | solution.py:12
  22.5 1.4 copy.8
  23.8 151.5 %all-to-all-done = f32[64,8,3072]{2,1,0:T(8,128)} async-done(((f32[64,8,3072]{2,1,0:T(8,128)}), f32[64,8,3072]{2,1,0:T(8,128)}, u32[]{:S(2)}, u32[]{:S(2)}) %all-to-all-start) | async-done | bytes 6291488 | tf_op jit(solution)/shard_map/all_to_all | solution.py:12
  175.3 1.8 slice.45
  177.2 4.7 %slice.43 = f32[512,2048]{1,0:T(8,128)} slice(f32[512,3072]{1,0:T(8,128)} %bitcast.6), slice={[0:512], [0:2048]} | slice | bytes 8388608 | tf_op jit(solution)/shard_map/slice | solution.py:18
  181.9 5.4 %copy.10 = f32[512,2048]{0,1:T(8,128)} copy(f32[512,2048]{1,0:T(8,128)} %slice.43) | data formatting | bytes 8388608 | tf_op jit(solution)/shard_map/reshape | solution.py:18
  187.3 1.8 copy.11
  189.1 2.8 slice_bitcast_fusion.2
  191.9 1.8 slice_bitcast_fusion
  195.2 225.3 %while.19 = (s32[]{:T(128)}, f32[1024,256]{0,1:T(8,128)}, f32[512,128]{0,1:T(8,128)}, f32[512,128]{0,1:T(8,128)}, s32[]{:T(128)}, /*index=5*/pred[]{:T(512)}, pr...) while((s32[]{:T(128)}, f32[1024,256]{0,1:T(8,128)}, ...), condition=%wide.region_3.4_spmd, body=%wide.region_0.3_spmd.sunk | while | flops 4027449344 | bytes 42992328 | solution.py:104
  195.2 3.6 collective-permute-start
  198.8 1.3 collective-permute-start.1
  200.1 1.7 select_dynamic-update-slice_fusion.2
  202.4 6.2 %collective-permute-start = (f32[512,128]{0,1:T(8,128)}, f32[512,128]{0,1:T(8,128)}, u32[]{:S(2)}, u32[]{:S(2)}) collective-permute-start(f32[512,128]{0,1:T(8,128)} %get-tuple-element.479), channel_id=1, source_target_pairs={{1,0},{2,1},{3,2},{4,3},{5,4},{6,5},{7,6},{9,8},{10,9},{11,10},{12... | collective-permute-start | bytes 786440 | tf_op jit(solution)/shard_map/while/body/eval_jaxpr/ppermute | solution.py:27
  208.6 1.3 collective-permute-start.1
  209.9 1.7 select_dynamic-update-slice_fusion.2
  211.7 11.0 %collective-permute-done.1 = f32[512,128]{0,1:T(8,128)S(1)} collective-permute-done((f32[512,128]{0,1:T(8,128)}, f32[512,128]{0,1:T(8,128)S(1)}, u32[]{:S(2)}, u32[]{:S(2)}) %collective-permute-start.1) | collective-permute-done | bytes 262176 | tf_op jit(solution)/shard_map/while/body/eval_jaxpr/ppermute | solution.py:27
  222.7 10.4 %collective-permute-start = (f32[512,128]{0,1:T(8,128)}, f32[512,128]{0,1:T(8,128)}, u32[]{:S(2)}, u32[]{:S(2)}) collective-permute-start(f32[512,128]{0,1:T(8,128)} %get-tuple-element.479), channel_id=1, source_target_pairs={{1,0},{2,1},{3,2},{4,3},{5,4},{6,5},{7,6},{9,8},{10,9},{11,10},{12... | collective-permute-start | bytes 786440 | tf_op jit(solution)/shard_map/while/body/eval_jaxpr/ppermute | solution.py:27
  234.4 1.7 select_dynamic-update-slice_fusion.2
  236.7 6.3 %collective-permute-start = (f32[512,128]{0,1:T(8,128)}, f32[512,128]{0,1:T(8,128)}, u32[]{:S(2)}, u32[]{:S(2)}) collective-permute-start(f32[512,128]{0,1:T(8,128)} %get-tuple-element.479), channel_id=1, source_target_pairs={{1,0},{2,1},{3,2},{4,3},{5,4},{6,5},{7,6},{9,8},{10,9},{11,10},{12... | collective-permute-start | bytes 786440 | tf_op jit(solution)/shard_map/while/body/eval_jaxpr/ppermute | solution.py:27
  244.4 1.7 select_dynamic-update-slice_fusion.2
  246.7 6.3 %collective-permute-start = (f32[512,128]{0,1:T(8,128)}, f32[512,128]{0,1:T(8,128)}, u32[]{:S(2)}, u32[]{:S(2)}) collective-permute-start(f32[512,128]{0,1:T(8,128)} %get-tuple-element.479), channel_id=1, source_target_pairs={{1,0},{2,1},{3,2},{4,3},{5,4},{6,5},{7,6},{9,8},{10,9},{11,10},{12... | collective-permute-start | bytes 786440 | tf_op jit(solution)/shard_map/while/body/eval_jaxpr/ppermute | solution.py:27
  254.3 1.7 select_dynamic-update-slice_fusion.2
  256.0 7.3 %collective-permute-done.1 = f32[512,128]{0,1:T(8,128)S(1)} collective-permute-done((f32[512,128]{0,1:T(8,128)}, f32[512,128]{0,1:T(8,128)S(1)}, u32[]{:S(2)}, u32[]{:S(2)}) %collective-permute-start.1) | collective-permute-done | bytes 262176 | tf_op jit(solution)/shard_map/while/body/eval_jaxpr/ppermute | solution.py:27
  263.3 28.4 %collective-permute-start = (f32[512,128]{0,1:T(8,128)}, f32[512,128]{0,1:T(8,128)}, u32[]{:S(2)}, u32[]{:S(2)}) collective-permute-start(f32[512,128]{0,1:T(8,128)} %get-tuple-element.479), channel_id=1, source_target_pairs={{1,0},{2,1},{3,2},{4,3},{5,4},{6,5},{7,6},{9,8},{10,9},{11,10},{12... | collective-permute-start | bytes 786440 | tf_op jit(solution)/shard_map/while/body/eval_jaxpr/ppermute | solution.py:27
  293.1 1.7 select_dynamic-update-slice_fusion.2
  294.8 10.7 %collective-permute-done.1 = f32[512,128]{0,1:T(8,128)S(1)} collective-permute-done((f32[512,128]{0,1:T(8,128)}, f32[512,128]{0,1:T(8,128)S(1)}, u32[]{:S(2)}, u32[]{:S(2)}) %collective-permute-start.1) | collective-permute-done | bytes 262176 | tf_op jit(solution)/shard_map/while/body/eval_jaxpr/ppermute | solution.py:27
  305.5 26.1 %collective-permute-start = (f32[512,128]{0,1:T(8,128)}, f32[512,128]{0,1:T(8,128)}, u32[]{:S(2)}, u32[]{:S(2)}) collective-permute-start(f32[512,128]{0,1:T(8,128)} %get-tuple-element.479), channel_id=1, source_target_pairs={{1,0},{2,1},{3,2},{4,3},{5,4},{6,5},{7,6},{9,8},{10,9},{11,10},{12... | collective-permute-start | bytes 786440 | tf_op jit(solution)/shard_map/while/body/eval_jaxpr/ppermute | solution.py:27
  332.9 1.7 select_dynamic-update-slice_fusion.2
  334.6 13.7 %collective-permute-done.1 = f32[512,128]{0,1:T(8,128)S(1)} collective-permute-done((f32[512,128]{0,1:T(8,128)}, f32[512,128]{0,1:T(8,128)S(1)}, u32[]{:S(2)}, u32[]{:S(2)}) %collective-permute-start.1) | collective-permute-done | bytes 262176 | tf_op jit(solution)/shard_map/while/body/eval_jaxpr/ppermute | solution.py:27
  348.4 23.0 %collective-permute-start = (f32[512,128]{0,1:T(8,128)}, f32[512,128]{0,1:T(8,128)}, u32[]{:S(2)}, u32[]{:S(2)}) collective-permute-start(f32[512,128]{0,1:T(8,128)} %get-tuple-element.479), channel_id=1, source_target_pairs={{1,0},{2,1},{3,2},{4,3},{5,4},{6,5},{7,6},{9,8},{10,9},{11,10},{12... | collective-permute-start | bytes 786440 | tf_op jit(solution)/shard_map/while/body/eval_jaxpr/ppermute | solution.py:27
  372.7 1.7 select_dynamic-update-slice_fusion.2
  375.0 15.0 %conditional.2 = ((f32[1024,256]{0,1:T(8,128)}, f32[512,128]{0,1:T(8,128)}, f32[512,128]{0,1:T(8,128)})) conditional(s32[]{:T(128)} %convert_element_type.11, (f32[1024,256]{0,1:T(8,128)}, f32[512,128]{0,1:T(8,128)}, f32[512,128]{0,1:T(8,128)}) %tuple.54, (pred[]{:T(512)}, s32[]{:T(128)}, f32[1024,256]{0,1:T(8,128)}, f32[512,128]{0,1:T(8,128)S(1)}, ...), branch_computations={%region_1.1_spmd, %region_2.2_spmd} | conditional | flops 4027383808 | bytes 40108272 | solution.py:101
  376.2 3.0 fusion.3
  380.5 2.3 fusion
  383.5 1.3 fusion.2
  386.0 2.3 constant_dynamic-update-slice_fusion
  390.0 6.2 %collective-permute-start = (f32[512,128]{0,1:T(8,128)}, f32[512,128]{0,1:T(8,128)}, u32[]{:S(2)}, u32[]{:S(2)}) collective-permute-start(f32[512,128]{0,1:T(8,128)} %get-tuple-element.479), channel_id=1, source_target_pairs={{1,0},{2,1},{3,2},{4,3},{5,4},{6,5},{7,6},{9,8},{10,9},{11,10},{12... | collective-permute-start | bytes 786440 | tf_op jit(solution)/shard_map/while/body/eval_jaxpr/ppermute | solution.py:27
  397.6 1.7 select_dynamic-update-slice_fusion.2
  399.9 15.0 %conditional.2 = ((f32[1024,256]{0,1:T(8,128)}, f32[512,128]{0,1:T(8,128)}, f32[512,128]{0,1:T(8,128)})) conditional(s32[]{:T(128)} %convert_element_type.11, (f32[1024,256]{0,1:T(8,128)}, f32[512,128]{0,1:T(8,128)}, f32[512,128]{0,1:T(8,128)}) %tuple.54, (pred[]{:T(512)}, s32[]{:T(128)}, f32[1024,256]{0,1:T(8,128)}, f32[512,128]{0,1:T(8,128)S(1)}, ...), branch_computations={%region_1.1_spmd, %region_2.2_spmd} | conditional | flops 4027383808 | bytes 40108272 | solution.py:101
  401.0 3.0 fusion.3
  405.3 2.3 fusion
  408.3 1.3 fusion.2
  410.8 2.3 constant_dynamic-update-slice_fusion
  414.9 2.0 collective-permute-start
  418.2 1.7 select_dynamic-update-slice_fusion.2
  420.5 2.5 copy.9
  (69 shorter events, 28.7 us)
Async XLA Ops:
  4.9 17.6 %copy-start.5 = (f32[1024,256]{1,0:T(8,128)S(1)}, f32[1024,256]{1,0:T(8,128)}, u32[]{:S(2)}) copy-start(f32[1024,256]{1,0:T(8,128)} %param.7) | copy-start | bytes 3145732
  4.9 170.4 %all-to-all-start = ((f32[64,8,3072]{2,1,0:T(8,128)}), f32[64,8,3072]{2,1,0:T(8,128)}, u32[]{:S(2)}, u32[]{:S(2)}) async-start(f32[64,8,3072]{2,1,0:T(8,128)} %stack.8), calls=%async_computation | async-start | bytes 12582912 | tf_op jit(solution)/shard_map/all_to_all | solution.py:12
  189.1 2.8 copy-start.4
  195.2 4.9 %collective-permute-start = (f32[512,128]{0,1:T(8,128)}, f32[512,128]{0,1:T(8,128)}, u32[]{:S(2)}, u32[]{:S(2)}) collective-permute-start(f32[512,128]{0,1:T(8,128)} %get-tuple-element.479), channel_id=1, source_target_pairs={{1,0},{2,1},{3,2},{4,3},{5,4},{6,5},{7,6},{9,8},{10,9},{11,10},{12... | collective-permute-start | bytes 786440 | tf_op jit(solution)/shard_map/while/body/eval_jaxpr/ppermute | solution.py:27
  198.8 3.6 collective-permute-start.1
  202.4 7.5 %collective-permute-start = (f32[512,128]{0,1:T(8,128)}, f32[512,128]{0,1:T(8,128)}, u32[]{:S(2)}, u32[]{:S(2)}) collective-permute-start(f32[512,128]{0,1:T(8,128)} %get-tuple-element.479), channel_id=1, source_target_pairs={{1,0},{2,1},{3,2},{4,3},{5,4},{6,5},{7,6},{9,8},{10,9},{11,10},{12... | collective-permute-start | bytes 786440 | tf_op jit(solution)/shard_map/while/body/eval_jaxpr/ppermute | solution.py:27
  208.6 14.1 %collective-permute-start.1 = (f32[512,128]{0,1:T(8,128)}, f32[512,128]{0,1:T(8,128)S(1)}, u32[]{:S(2)}, u32[]{:S(2)}) collective-permute-start(f32[512,128]{0,1:T(8,128)} %get-tuple-element.478), channel_id=1, source_target_pairs={{0,1},{1,2},{2,3},{3,4},{4,5},{5,6},{6,7},{8,9},{9,10},{10,11},{11... | collective-permute-start | bytes 786440 | tf_op jit(solution)/shard_map/while/body/eval_jaxpr/ppermute | solution.py:27
  222.7 11.7 %collective-permute-start = (f32[512,128]{0,1:T(8,128)}, f32[512,128]{0,1:T(8,128)}, u32[]{:S(2)}, u32[]{:S(2)}) collective-permute-start(f32[512,128]{0,1:T(8,128)} %get-tuple-element.479), channel_id=1, source_target_pairs={{1,0},{2,1},{3,2},{4,3},{5,4},{6,5},{7,6},{9,8},{10,9},{11,10},{12... | collective-permute-start | bytes 786440 | tf_op jit(solution)/shard_map/while/body/eval_jaxpr/ppermute | solution.py:27
  233.1 3.6 collective-permute-start.1
  236.7 7.6 %collective-permute-start = (f32[512,128]{0,1:T(8,128)}, f32[512,128]{0,1:T(8,128)}, u32[]{:S(2)}, u32[]{:S(2)}) collective-permute-start(f32[512,128]{0,1:T(8,128)} %get-tuple-element.479), channel_id=1, source_target_pairs={{1,0},{2,1},{3,2},{4,3},{5,4},{6,5},{7,6},{9,8},{10,9},{11,10},{12... | collective-permute-start | bytes 786440 | tf_op jit(solution)/shard_map/while/body/eval_jaxpr/ppermute | solution.py:27
  243.0 3.6 collective-permute-start.1
  246.7 7.6 %collective-permute-start = (f32[512,128]{0,1:T(8,128)}, f32[512,128]{0,1:T(8,128)}, u32[]{:S(2)}, u32[]{:S(2)}) collective-permute-start(f32[512,128]{0,1:T(8,128)} %get-tuple-element.479), channel_id=1, source_target_pairs={{1,0},{2,1},{3,2},{4,3},{5,4},{6,5},{7,6},{9,8},{10,9},{11,10},{12... | collective-permute-start | bytes 786440 | tf_op jit(solution)/shard_map/while/body/eval_jaxpr/ppermute | solution.py:27
  252.9 10.4 %collective-permute-start.1 = (f32[512,128]{0,1:T(8,128)}, f32[512,128]{0,1:T(8,128)S(1)}, u32[]{:S(2)}, u32[]{:S(2)}) collective-permute-start(f32[512,128]{0,1:T(8,128)} %get-tuple-element.478), channel_id=1, source_target_pairs={{0,1},{1,2},{2,3},{3,4},{4,5},{5,6},{6,7},{8,9},{9,10},{10,11},{11... | collective-permute-start | bytes 786440 | tf_op jit(solution)/shard_map/while/body/eval_jaxpr/ppermute | solution.py:27
  263.3 29.7 %collective-permute-start = (f32[512,128]{0,1:T(8,128)}, f32[512,128]{0,1:T(8,128)}, u32[]{:S(2)}, u32[]{:S(2)}) collective-permute-start(f32[512,128]{0,1:T(8,128)} %get-tuple-element.479), channel_id=1, source_target_pairs={{1,0},{2,1},{3,2},{4,3},{5,4},{6,5},{7,6},{9,8},{10,9},{11,10},{12... | collective-permute-start | bytes 786440 | tf_op jit(solution)/shard_map/while/body/eval_jaxpr/ppermute | solution.py:27
  291.8 13.8 %collective-permute-start.1 = (f32[512,128]{0,1:T(8,128)}, f32[512,128]{0,1:T(8,128)S(1)}, u32[]{:S(2)}, u32[]{:S(2)}) collective-permute-start(f32[512,128]{0,1:T(8,128)} %get-tuple-element.478), channel_id=1, source_target_pairs={{0,1},{1,2},{2,3},{3,4},{4,5},{5,6},{6,7},{8,9},{9,10},{10,11},{11... | collective-permute-start | bytes 786440 | tf_op jit(solution)/shard_map/while/body/eval_jaxpr/ppermute | solution.py:27
  305.5 27.4 %collective-permute-start = (f32[512,128]{0,1:T(8,128)}, f32[512,128]{0,1:T(8,128)}, u32[]{:S(2)}, u32[]{:S(2)}) collective-permute-start(f32[512,128]{0,1:T(8,128)} %get-tuple-element.479), channel_id=1, source_target_pairs={{1,0},{2,1},{3,2},{4,3},{5,4},{6,5},{7,6},{9,8},{10,9},{11,10},{12... | collective-permute-start | bytes 786440 | tf_op jit(solution)/shard_map/while/body/eval_jaxpr/ppermute | solution.py:27
  331.6 16.8 %collective-permute-start.1 = (f32[512,128]{0,1:T(8,128)}, f32[512,128]{0,1:T(8,128)S(1)}, u32[]{:S(2)}, u32[]{:S(2)}) collective-permute-start(f32[512,128]{0,1:T(8,128)} %get-tuple-element.478), channel_id=1, source_target_pairs={{0,1},{1,2},{2,3},{3,4},{4,5},{5,6},{6,7},{8,9},{9,10},{10,11},{11... | collective-permute-start | bytes 786440 | tf_op jit(solution)/shard_map/while/body/eval_jaxpr/ppermute | solution.py:27
  348.4 24.4 %collective-permute-start = (f32[512,128]{0,1:T(8,128)}, f32[512,128]{0,1:T(8,128)}, u32[]{:S(2)}, u32[]{:S(2)}) collective-permute-start(f32[512,128]{0,1:T(8,128)} %get-tuple-element.479), channel_id=1, source_target_pairs={{1,0},{2,1},{3,2},{4,3},{5,4},{6,5},{7,6},{9,8},{10,9},{11,10},{12... | collective-permute-start | bytes 786440 | tf_op jit(solution)/shard_map/while/body/eval_jaxpr/ppermute | solution.py:27
  371.4 3.6 collective-permute-start.1
  375.0 4.2 copy-start.1
  376.2 4.2 %copy-start = (f32[1024,512]{1,0:T(8,128)S(1)}, f32[1024,512]{1,0:T(8,128)}, u32[]{:S(2)}) copy-start(f32[1024,512]{1,0:T(8,128)} %get-tuple-element.301) | copy-start | bytes 6291460 | tf_op jit(solution)/shard_map/while/body/eval_jaxpr/cond
  383.5 2.5 copy-start.2
  388.3 1.0 copy-start.3
  390.0 7.5 %collective-permute-start = (f32[512,128]{0,1:T(8,128)}, f32[512,128]{0,1:T(8,128)}, u32[]{:S(2)}, u32[]{:S(2)}) collective-permute-start(f32[512,128]{0,1:T(8,128)} %get-tuple-element.479), channel_id=1, source_target_pairs={{1,0},{2,1},{3,2},{4,3},{5,4},{6,5},{7,6},{9,8},{10,9},{11,10},{12... | collective-permute-start | bytes 786440 | tf_op jit(solution)/shard_map/while/body/eval_jaxpr/ppermute | solution.py:27
  396.2 3.6 collective-permute-start.1
  399.9 4.2 copy-start.1
  401.0 4.2 %copy-start = (f32[1024,512]{1,0:T(8,128)S(1)}, f32[1024,512]{1,0:T(8,128)}, u32[]{:S(2)}) copy-start(f32[1024,512]{1,0:T(8,128)} %get-tuple-element.301) | copy-start | bytes 6291460 | tf_op jit(solution)/shard_map/while/body/eval_jaxpr/cond
  408.3 2.5 copy-start.2
  413.1 1.0 copy-start.3
  414.9 3.3 collective-permute-start
  416.9 3.6 collective-permute-start.1
